TPU v7x, 32 devices: a whole 2x2x4 slice. The times are simulated.
32 devices in a mesh: dp: 8 (over y, x, core), mp: 4 (over z).
Axes of the slice: x: 2, y: 2, z: 4, core: 2. Of those that a mesh axis runs over, the one named last changes fastest.
Arguments:
- tokens: bfloat16 [8192, 2048], P('dp'), may hold values from -6 to 6
- cotangent: bfloat16 [8192, 2048], P('dp'), may hold values from -6 to 6
- counts: int32 [8], replicated, may hold values from 1 to 1024, 5120 in all
- w_qkv: bfloat16 [2048, 3, 2048], P('dp', None, 'mp'), may hold values from -0.125 to 0.125
- w_out: bfloat16 [2048, 2048], P('mp', 'dp'), may hold values from -1 to 1
- w_fc1: bfloat16 [2048, 8192], P('dp', 'mp'), may hold values from -0.125 to 0.125
- w_fc2: bfloat16 [8192, 2048], P('mp', 'dp'), may hold values from -0.0625 to 0.0625
- ln1_gain: bfloat16 [2048], P('dp'), may hold values from 0.5 to 1.5
- ln1_bias: bfloat16 [2048], P('dp'), may hold values from -1.796875 to 1.796875
- ln2_gain: bfloat16 [2048], P('dp'), may hold values from 0.5 to 1.5
- ln2_bias: bfloat16 [2048], P('dp'), may hold values from -1.796875 to 1.796875
- qv_bias: bfloat16 [2, 2048], P(None, ('mp', 'dp')), may hold values from -1.796875 to 1.796875
- out_bias: bfloat16 [2048], P('dp'), may hold values from -1.796875 to 1.796875
- fc1_bias: bfloat16 [8192], P(('mp', 'dp')), may hold values from -1.796875 to 1.796875
- fc2_bias: bfloat16 [2048], P('dp'), may hold values from -1.796875 to 1.796875
Outputs:
- out_tokens: bfloat16 [8192, 2048], P('dp')
- grad_tokens: float32 [8192, 2048], P('dp')
- grad_w_qkv: float32 [2048, 3, 2048], P('dp', None, 'mp')
- grad_w_out: float32 [2048, 2048], P('mp', 'dp')
- grad_w_fc1: float32 [2048, 8192], P('dp', 'mp')
- grad_w_fc2: float32 [8192, 2048], P('mp', 'dp')
- grad_ln1_gain: float32 [2048], P('dp')
- grad_ln1_bias: float32 [2048], P('dp')
- grad_ln2_gain: float32 [2048], P('dp')
- grad_ln2_bias: float32 [2048], P('dp')
- grad_qv_bias: float32 [2, 2048], P(None, ('mp', 'dp'))
- grad_out_bias: float32 [2048], P('dp')
- grad_fc1_bias: float32 [8192], P(('mp', 'dp'))
- grad_fc2_bias: float32 [2048], P('dp')
Inputs may be any that keep to these rules, and one draw needn't show every extreme that they name: counts[g] is the number of live tokens of group g's sequence, at the start of its 1024 slots; the largest count equals 1024.
All inputs are finite; a program needn't handle non-finite values.
Results may differ from a plain program's by a relative error of at most 0.014.
Values may be sent and summed in bfloat16 or wider, within the bound.
A program may use at most 192 MiB of HBM per device.

v0:
```python
import math
import jax
import jax.numpy as jnp
from jax import lax
from jax.sharding import PartitionSpec as P

HEAD = 128
EPS = 1e-05
NEG = -1e30


def layer_norm(values, gain_vec, shift_vec):
    center = values - jnp.mean(values, axis=-1, keepdims=True)
    spread = jnp.mean(center * center, axis=-1, keepdims=True)
    return center * lax.rsqrt(spread + EPS) * gain_vec + shift_vec


def smooth_gate(values):
    return jax.nn.gelu(values, approximate=True)


def causal_scores(queries, key_heads, inv_root):
    row_count = queries.shape[0]
    raw_scores = (
        jnp.einsum("qhd,khd->hqk", queries, key_heads, preferred_element_type=jnp.float32)
        * inv_root
    )
    future = lax.broadcasted_iota(jnp.int32, (row_count, row_count), 1) > lax.broadcasted_iota(
        jnp.int32, (row_count, row_count), 0
    )
    return jnp.where(future[None], NEG, raw_scores)


def shards(
    tokens,
    cotangent,
    counts,
    w_qkv,
    w_out,
    w_fc1,
    w_fc2,
    ln1_gain,
    ln1_bias,
    ln2_gain,
    ln2_bias,
    qv_bias,
    out_bias,
    fc1_bias,
    fc2_bias,
):
    whole_qkv = lax.all_gather(w_qkv, "dp", axis=0, tiled=True)
    whole_out = lax.all_gather(w_out, "dp", axis=1, tiled=True)
    whole_fc1 = lax.all_gather(w_fc1, "dp", axis=0, tiled=True)
    whole_fc2 = lax.all_gather(w_fc2, "dp", axis=1, tiled=True)
    vectors = (
        ln1_gain,
        ln1_bias,
        ln2_gain,
        ln2_bias,
        out_bias,
        fc2_bias,
        fc1_bias,
        qv_bias.reshape(-1),
    )
    packed = lax.all_gather(jnp.concatenate(vectors), "dp", axis=0).astype(jnp.float32)
    wide = []
    at = 0
    for vector in vectors:
        wide.append(packed[:, at : at + vector.shape[0]])
        at += vector.shape[0]
    gain_one, shift_one, gain_two, shift_two, bias_out, bias_fc2, bias_fc1 = (
        part.reshape(-1) for part in wide[:7]
    )
    n_dp = packed.shape[0]
    bias_qv = wide[7].reshape(n_dp, 2, -1).transpose(1, 0, 2).reshape(2, -1)
    seq_rows = tokens.shape[0]
    local_width = whole_qkv.shape[2]
    heads_here = local_width // HEAD
    inv_root = 1.0 / math.sqrt(HEAD)
    inputs = tokens.astype(jnp.float32)
    normed_one = layer_norm(inputs, gain_one, shift_one).astype(jnp.bfloat16)
    projected = jnp.einsum("sd,dce->sce", normed_one, whole_qkv, preferred_element_type=jnp.float32)
    queries = (
        (projected[:, 0] + bias_qv[0]).astype(jnp.bfloat16).reshape(seq_rows, heads_here, HEAD)
    )
    key_heads = projected[:, 1].astype(jnp.bfloat16).reshape(seq_rows, heads_here, HEAD)
    values = (projected[:, 2] + bias_qv[1]).astype(jnp.bfloat16).reshape(seq_rows, heads_here, HEAD)
    scores = causal_scores(queries, key_heads, inv_root)
    row_peak = jnp.max(scores, axis=-1, keepdims=True)
    exp_terms = jnp.exp(scores - row_peak)
    exp_total = jnp.sum(exp_terms, axis=-1, keepdims=True)
    log_total = row_peak + jnp.log(exp_total)
    prob_low = (exp_terms / exp_total).astype(jnp.bfloat16)
    mixed_heads = (
        jnp.einsum("hqk,khd->qhd", prob_low, values, preferred_element_type=jnp.float32)
        .astype(jnp.bfloat16)
        .reshape(seq_rows, local_width)
    )
    attn_part = jnp.dot(mixed_heads, whole_out, preferred_element_type=jnp.float32)
    residual = (
        inputs + lax.psum(attn_part.astype(jnp.bfloat16), "mp").astype(jnp.float32) + bias_out
    )
    normed_two = layer_norm(residual, gain_two, shift_two).astype(jnp.bfloat16)
    preact = jnp.dot(normed_two, whole_fc1, preferred_element_type=jnp.float32) + bias_fc1
    activated = smooth_gate(preact).astype(jnp.bfloat16)
    ffn_part = jnp.dot(activated, whole_fc2, preferred_element_type=jnp.float32)
    out_tokens = (
        residual + lax.psum(ffn_part.astype(jnp.bfloat16), "mp").astype(jnp.float32) + bias_fc2
    ).astype(jnp.bfloat16)
    dp_index = lax.axis_index("dp")
    slot_ids = lax.iota(jnp.int32, counts.shape[0])
    own_count = jnp.sum(jnp.where(slot_ids == dp_index, counts, 0))
    weight_share = own_count.astype(jnp.float32) / jnp.sum(counts).astype(jnp.float32)
    live_rows = lax.iota(jnp.int32, seq_rows) < own_count
    grad_out = jnp.where(live_rows[:, None], cotangent.astype(jnp.float32), 0.0)
    grad_out_low = grad_out.astype(jnp.bfloat16)
    grad_fc2 = (
        jnp.einsum("sf,sd->fd", activated, grad_out_low, preferred_element_type=jnp.float32)
        * weight_share
    )
    grad_fc2_bias = jnp.sum(grad_out, axis=0) * weight_share
    delta_act = jnp.einsum("sd,fd->sf", grad_out_low, whole_fc2, preferred_element_type=jnp.float32)
    unused_gate, gate_back = jax.vjp(smooth_gate, preact)
    delta_pre = gate_back(delta_act)[0]
    grad_fc1_bias = jnp.sum(delta_pre, axis=0) * weight_share
    delta_pre_low = delta_pre.astype(jnp.bfloat16)
    grad_fc1 = (
        jnp.einsum("sd,sf->df", normed_two, delta_pre_low, preferred_element_type=jnp.float32)
        * weight_share
    )
    two_part = jnp.einsum("sf,df->sd", delta_pre_low, whole_fc1, preferred_element_type=jnp.float32)
    delta_two = lax.psum(two_part.astype(jnp.bfloat16), "mp").astype(jnp.float32)
    unused_two, second_back = jax.vjp(layer_norm, residual, gain_two, shift_two)
    resid_part, gain_two_part, shift_two_part = second_back(delta_two)
    delta_resid = resid_part + grad_out
    delta_resid_low = delta_resid.astype(jnp.bfloat16)
    out_bias_part = jnp.sum(delta_resid, axis=0)
    grad_out_proj = (
        jnp.einsum("sc,sd->cd", mixed_heads, delta_resid_low, preferred_element_type=jnp.float32)
        * weight_share
    )
    delta_mixed = jnp.einsum(
        "sd,cd->sc", delta_resid_low, whole_out, preferred_element_type=jnp.float32
    )
    delta_mixed_low = delta_mixed.astype(jnp.bfloat16).reshape(seq_rows, heads_here, HEAD)
    scores_again = causal_scores(queries, key_heads, inv_root)
    prob_full = jnp.exp(scores_again - log_total)
    delta_prob = jnp.einsum(
        "qhd,khd->hqk", delta_mixed_low, values, preferred_element_type=jnp.float32
    )
    delta_scores = prob_full * (
        delta_prob - jnp.sum(prob_full * delta_prob, axis=-1, keepdims=True)
    )
    delta_scores_low = delta_scores.astype(jnp.bfloat16)
    delta_q = (
        jnp.einsum("hqk,khd->qhd", delta_scores_low, key_heads, preferred_element_type=jnp.float32)
        * inv_root
    ).reshape(seq_rows, local_width)
    delta_k = (
        jnp.einsum("hqk,qhd->khd", delta_scores_low, queries, preferred_element_type=jnp.float32)
        * inv_root
    ).reshape(seq_rows, local_width)
    delta_v = jnp.einsum(
        "hqk,qhd->khd", prob_low, delta_mixed_low, preferred_element_type=jnp.float32
    ).reshape(seq_rows, local_width)
    grad_qv = jnp.stack([jnp.sum(delta_q, axis=0), jnp.sum(delta_v, axis=0)]) * weight_share
    delta_proj = jnp.stack([delta_q, delta_k, delta_v], axis=1).astype(jnp.bfloat16)
    grad_qkv = (
        jnp.einsum("sd,sce->dce", normed_one, delta_proj, preferred_element_type=jnp.float32)
        * weight_share
    )
    one_part = jnp.einsum("sce,dce->sd", delta_proj, whole_qkv, preferred_element_type=jnp.float32)
    delta_one = lax.psum(one_part.astype(jnp.bfloat16), "mp").astype(jnp.float32)
    unused_one, first_back = jax.vjp(layer_norm, inputs, gain_one, shift_one)
    input_part, gain_one_part, shift_one_part = first_back(delta_one)
    grad_tokens = input_part + delta_resid
    grad_vectors = (
        gain_one_part * weight_share,
        shift_one_part * weight_share,
        gain_two_part * weight_share,
        shift_two_part * weight_share,
        out_bias_part * weight_share,
        grad_fc2_bias,
        grad_fc1_bias,
    )
    stacked = jnp.concatenate(
        [vector.reshape(n_dp, -1) for vector in grad_vectors]
        + [grad_qv.reshape(2, n_dp, -1).transpose(1, 0, 2).reshape(n_dp, -1)],
        axis=1,
    )
    own = lax.psum_scatter(stacked, "dp", scatter_dimension=0, tiled=True)[0]
    pieces = []
    at = 0
    for vector in vectors:
        pieces.append(own[at : at + vector.shape[0]])
        at += vector.shape[0]

    def scatter(grad, axis):
        low = grad.astype(jnp.bfloat16)
        return lax.psum_scatter(low, "dp", scatter_dimension=axis, tiled=True).astype(jnp.float32)

    return (
        out_tokens,
        grad_tokens,
        scatter(grad_qkv, 0),
        scatter(grad_out_proj, 1),
        scatter(grad_fc1, 0),
        scatter(grad_fc2, 1),
        pieces[0],
        pieces[1],
        pieces[2],
        pieces[3],
        pieces[7].reshape(2, -1),
        pieces[4],
        pieces[6],
        pieces[5],
    )


def solution(mesh):
    placed = (
        P("dp", None),
        P("dp", None),
        P(),
        P("dp", None, "mp"),
        P("mp", "dp"),
        P("dp", "mp"),
        P("mp", "dp"),
        P("dp"),
        P("dp"),
        P("dp"),
        P("dp"),
        P(None, ("mp", "dp")),
        P("dp"),
        P(("mp", "dp")),
        P("dp"),
    )
    return jax.shard_map(
        shards,
        mesh=mesh,
        in_specs=placed,
        out_specs=(
            P("dp", None),
            P("dp", None),
            P("dp", None, "mp"),
            P("mp", "dp"),
            P("dp", "mp"),
            P("mp", "dp"),
            P("dp"),
            P("dp"),
            P("dp"),
            P("dp"),
            P(None, ("mp", "dp")),
            P("dp"),
            P(("mp", "dp")),
            P("dp"),
        ),
        check_vma=False,
    )
```

profile of v0, /device:TPU:0, one launch (start us, length us, event | category | flops | bytes accessed | tf_op | source)
XLA Modules:
  0.0 1186.2 jit_solution(16017044724826769908)
XLA Ops:
  7.2 2.3 copy.59
  11.1 0.8 dynamic-update-slice.8
  11.9 0.8 dynamic-update-slice.9
  12.8 0.8 dynamic-update-slice.10
  13.6 0.8 dynamic-update-slice.11
  14.4 0.8 dynamic-update-slice.12
  15.2 0.8 dynamic-update-slice.13
  17.1 11.2 all-gather.1
  29.2 2.8 convert_reduce_fusion.2
  32.0 1.2 fusion.18
  33.9 26.1 %all-gather.7.cloned.1.call-done = bf16[2048,3,512]{0,2,1:T(8,128)(2,1)} async-done(((bf16[256,3,512]{0,2,1:T(8,128)(2,1)}), bf16[2048,3,512]{0,2,1:T(8,128)(2,1)}) %all-gather.7.cloned.1.call-update) | async-done | bytes 6291472 | tf_op jit(solution)/shard_map/all_gather | solution.py:51
  60.0 10.4 fusion.43
  70.6 1.7 fusion.60
  72.3 7.7 fusion.62
  80.0 8.1 fusion
  88.1 2.0 copy.60
  90.1 7.4 divide_convert_fusion
  97.6 3.2 copy-done.6
  100.8 1.4 convolution_convert_fusion.3
  102.3 6.0 convolution_convert_fusion.2
  110.9 152.8 %all-reduce.6.cloned.1.call-done = bf16[1024,2048]{1,0:T(8,128)(2,1)} async-done(((bf16[1024,2048]{1,0:T(8,128)(2,1)}), bf16[1024,2048]{1,0:T(8,128)(2,1)}) %all-reduce.6.cloned.1.call-update) | async-done | bytes 4194320 | tf_op jit(solution)/shard_map/psum | solution.py:101
  263.7 5.0 fusion.26
  268.7 0.9 copy-done.4
  269.6 2.4 multiply_reduce_fusion.1
  272.0 46.6 %all-gather.11.cloned.1.call-done = bf16[2048,2048]{1,0:T(8,128)(2,1)} async-done(((bf16[256,2048]{1,0:T(8,128)(2,1)}), bf16[2048,2048]{1,0:T(8,128)(2,1)}) %all-gather.11.cloned.1.call-update) | async-done | bytes 8388624 | tf_op jit(solution)/shard_map/all_gather | solution.py:53
  318.7 16.2 %fusion.55 = f32[1024,2048]{1,0:T(8,128)} fusion(bf16[2048,2048]{1,0:T(8,128)(2,1)} %all-gather.11.cloned.1.call-done, f32[2048]{0:T(1024)S(1)} %bitcast.118, f32[2048]{0:T(1024)S(1)} %bitcast.109, f32[1024]{0:T(1024)S(1)} %fusion.48, bf16[1024,2048]{1,0:T(8,128)(2,1)} %all-reduce.6.cloned.1.call-done, bf16[1024,2048]{1,0:T(8,128)(2,1)} %param.15, ...), kind=kOutput, calls=%fused_computation.131 | convolution fusion | flops 8608808960 | bytes 25198592 | tf_op jit(solution)/shard_map/dot_general | solution.py:104
  334.8 41.4 %all-gather.13.cloned.1.call-done = bf16[2048,2048]{1,0:T(8,128)(2,1)} async-done(((bf16[2048,256]{1,0:T(8,128)(2,1)}), bf16[2048,2048]{1,0:T(8,128)(2,1)}) %all-gather.13.cloned.1.call-update) | async-done | bytes 8388624 | tf_op jit(solution)/shard_map/all_gather | solution.py:54
  376.3 20.5 %fusion.63 = (f32[2048]{0:T(1024)}, bf16[1024,2048]{1,0:T(8,128)(2,1)S(1)}) fusion(f32[1024,2048]{1,0:T(8,128)} %fusion.55, f32[2048]{0:T(1024)S(1)} %bitcast.120, bf16[2048,2048]{1,0:T(8,128)(2,1)} %all-gather.13.cloned.1.call-done, bf16[1024,2048]{1,0:T(8,128)(2,1)} %param.16, pred[1024]{0:T(1024)(128)(4,1)S(1)} %iota_compare_fusion.1), kind=kOutput, calls=%fused_computation.137 | convolution fusion | flops 8642361344 | bytes 25183232 | tf_op jit(solution)/shard_map/sd,fd->sf/dot_general | solution.py:122
  396.8 2.0 copy-done.38
  398.8 23.0 %convolution_convert_fusion = bf16[1024,2048]{1,0:T(8,128)(2,1)} fusion(bf16[2048,2048]{1,0:T(8,128)(2,1)} %all-gather.11.cloned.1.call-done, bf16[1024,2048]{1,0:T(8,128)(2,1)S(1)} %get-tuple-element.58), kind=kOutput, calls=%fused_computation.61 | convolution fusion | flops 8592031744 | bytes 16777216 | tf_op jit(solution)/shard_map/sf,df->sd/dot_general | solution.py:131
  423.2 16.6 %convolution_convert_fusion.1 = bf16[1024,2048]{1,0:T(8,128)(2,1)} fusion(bf16[2048,2048]{1,0:T(8,128)(2,1)} %all-gather.13.cloned.1.call-done, f32[1024,2048]{1,0:T(8,128)} %fusion.55, f32[2048]{0:T(1024)S(1)} %bitcast.121), kind=kOutput, calls=%fused_computation.62 | convolution fusion | flops 8613003264 | bytes 20979712 | tf_op jit(solution)/shard_map/dot_general | solution.py:106
  439.8 137.2 %all-reduce.8.cloned.1.call-done = bf16[1024,2048]{1,0:T(8,128)(2,1)} async-done(((bf16[1024,2048]{1,0:T(8,128)(2,1)}), bf16[1024,2048]{1,0:T(8,128)(2,1)}) %all-reduce.8.cloned.1.call-update) | async-done | bytes 4194320 | tf_op jit(solution)/shard_map/psum | solution.py:132
  577.0 7.6 convert_reduce_fusion.1
  585.3 5.5 fusion.21
  590.8 5.7 fusion.59
  596.5 3.2 copy-done.9
  599.7 3.7 multiply_convert_fusion.5
  603.8 6.3 fusion.39
  610.2 12.3 %multiply_reduce_fusion = (f32[4,1024]{1,0:T(4,128)S(1)}, f32[4,1024,1024]{1,2,0:T(8,128)}) fusion(f32[4,1024,1024]{1,2,0:T(8,128)} %get-tuple-element.50, f32[4,1024]{1,0:T(4,128)S(1)} %log_add_fusion, bf16[1024,4,128]{0,2,1:T(8,128)(2,1)S(1)} %bitcast.87, f32[1024,4,128]{2,0,1:T(8,128)S(1)} %copy.60, f32[4,128]{1,0:T(4,128)S(1)} %add.145), kind=kOutput, calls=%fused_computation.3 | convolution fusion | flops 1087369216 | bytes 36734976 | tf_op jit(solution)/shard_map/qhd,khd->hqk/dot_general | solution.py:148
  622.4 15.9 %multiply_convert_fusion.2 = bf16[4,1024,1024]{1,2,0:T(8,128)(2,1)} fusion(f32[4,1024,1024]{1,2,0:T(8,128)} %get-tuple-element.54, f32[4,1024,1024]{1,2,0:T(8,128)} %get-tuple-element.50, f32[4,1024]{1,0:T(4,128)S(1)} %get-tuple-element.53, f32[4,1024]{1,0:T(4,128)S(1)} %log_add_fusion), kind=kLoop, calls=%fused_computation.2 | loop fusion | flops 16777216 | bytes 41975808 | tf_op jit(solution)/shard_map/convert_element_type | solution.py:154
  638.4 4.6 bitcast_convert_fusion.1
  642.9 2.5 copy.71
  645.5 6.4 bitcast_convert_fusion.2
  651.8 2.3 copy.69
  654.1 6.3 multiply_convert_fusion.6
  660.9 11.0 bitcast_convert_fusion
  672.0 16.4 %multiply_convert_fusion = bf16[2048,2048]{1,0:T(8,128)(2,1)} fusion(f32[]{:T(128)S(6)} %div.63, bf16[1024,2048]{1,0:T(8,128)(2,1)} %param.16, pred[1024]{0:T(1024)(128)(4,1)S(1)} %iota_compare_fusion.1, f32[1024,2048]{1,0:T(8,128)} %fusion.55, f32[2048]{0:T(1024)S(1)} %bitcast.122), kind=kOutput, calls=%fused_computation | convolution fusion | flops 8625586176 | bytes 20980740 | tf_op jit(solution)/shard_map/sf,sd->fd/dot_general | solution.py:118
  689.2 15.5 %multiply_convert_fusion.1 = bf16[2048,2048]{1,0:T(8,128)(2,1)} fusion(f32[]{:T(128)S(6)} %div.63, bf16[1024,2048]{1,0:T(8,128)(2,1)} %copy-done.38, f32[2048]{0:T(1024)S(1)} %bitcast.119, f32[2048]{0:T(1024)S(1)} %bitcast.113, f32[1024]{0:T(1024)S(1)} %fusion.48, bf16[1024,2048]{1,0:T(8,128)(2,1)} %all-reduce.6.cloned.1.call-done, ...), kind=kOutput, calls=%fused_computation.1 | convolution fusion | flops 8617197568 | bytes 21004292 | tf_op jit(solution)/shard_map/sd,sf->df/dot_general | solution.py:128
  704.8 1.1 copy-done.16
  706.6 12.6 %multiply_convert_fusion.3 = bf16[2048,3,512]{2,0,1:T(8,128)(2,1)} fusion(f32[]{:T(128)S(6)} %div.63, bf16[1024,1,512]{2,0,1:T(8,128)(2,1)S(1)} %copy-done.16, bf16[1024,1,512]{2,0,1:T(8,128)(2,1)S(1)} %copy-done.19, bf16[1024,1,512]{2,0,1:T(8,128)(2,1)S(1)} %copy-done.17, bf16[1024,2048]{1,0:T(8,128)(2,1)} %param.15, f32[2048]{0:T(1024)S(1)} %bitcast.117, ...), kind=kOutput, calls=%fused_computation.9 | convolution fusion | flops 6470762496 | bytes 13656068 | tf_op jit(solution)/shard_map/sd,sce->dce/dot_general | solution.py:169
  719.9 1.8 bitcast_reduce_fusion
  722.2 1.8 convert_element_type.144
  724.0 238.4 %all-reduce.10.cloned.1.call-done = (bf16[1024,2048]{1,0:T(8,128)(2,1)}, bf16[1024,2048]{1,0:T(8,128)(2,1)}) async-done(((bf16[1024,2048]{1,0:T(8,128)(2,1)}, bf16[1024,2048]{1,0:T(8,128)(2,1)}), (bf16[1024,2048]{1,0:T(8,128)(2,1)}, bf16[1024,2048]{1,0:T(8,128)(2,1)})) %all-reduce.10.cloned.1.call-update) | async-done | bytes 8388624 | tf_op jit(solution)/shard_map/psum | solution.py:108
  962.3 5.5 convert_reduce_fusion
  968.3 4.5 fusion.22
  972.8 25.3 %all-reduce = f32[8,1920]{1,0:T(8,128)S(1)} all-reduce(f32[8,1920]{1,0:T(8,128)S(1)} %constant_dynamic-update-slice_fusion), channel_id=7, replica_groups=mesh['dp'=8,'mp'=4] {'dp'}, use_global_device_ids=true, to_apply=%region_30.31.clone | all-reduce | flops 15360 | bytes 122880
  999.5 36.7 %reduce-scatter.11.cloned.1.call-done = bf16[2048,256]{1,0:T(8,128)(2,1)} async-done(((bf16[2048,2048]{1,0:T(8,128)(2,1)}), bf16[2048,256]{1,0:T(8,128)(2,1)}) %reduce-scatter.11.cloned.1.call-update) | async-done | bytes 1048592 | tf_op jit(solution)/shard_map/reduce_scatter | solution.py:200
  1036.3 2.7 convert_element_type.148
  1039.0 72.7 %reduce-scatter.9.cloned.1.call-done = bf16[256,2048]{1,0:T(8,128)(2,1)} async-done(((bf16[2048,2048]{1,0:T(8,128)(2,1)}), bf16[256,2048]{1,0:T(8,128)(2,1)}) %reduce-scatter.9.cloned.1.call-update) | async-done | bytes 1048592 | tf_op jit(solution)/shard_map/reduce_scatter | solution.py:200
  1111.7 2.8 convert_element_type.146
  1114.5 1.3 fusion.61
  1115.8 17.6 %add_add_fusion.2 = (f32[1024,2048]{1,0:T(8,128)}, bf16[1024,2048]{1,0:T(8,128)(2,1)}) fusion(f32[1024,2048]{1,0:T(8,128)} %copy-done.9, bf16[1024,2048]{1,0:T(8,128)(2,1)} %param.15, bf16[1024,2048]{1,0:T(8,128)(2,1)} %get-tuple-element.27, f32[1024]{0:T(1024)S(1)} %negate_multiply_fusion, f32[1024]{0:T(1024)S(1)} %multiply_multiply_fusion.2, ...), kind=kLoop, calls=%fused_computation.46 | loop fusion | flops 35651584 | bytes 37789696 | tf_op jit(solution)/shard_map/add | solution.py:176
  1133.4 43.3 %reduce-scatter.5.cloned.1.call-done = bf16[256,3,512]{2,0,1:T(8,128)(2,1)} async-done(((bf16[2048,3,512]{2,0,1:T(8,128)(2,1)}), bf16[256,3,512]{2,0,1:T(8,128)(2,1)}) %reduce-scatter.5.cloned.1.call-update) | async-done | bytes 786448 | tf_op jit(solution)/shard_map/reduce_scatter | solution.py:200
  1176.7 2.5 convert_element_type.142
  (162 shorter events, 13.1 us)
Async XLA Ops:
  7.2 52.8 %all-gather.7.cloned.1.call-start = ((), (), s32[]{:S(2)}) async-start(), calls=%async_computation.4 | async-start | bytes 7077888 | tf_op jit(solution)/shard_map/all_gather | solution.py:51
  9.5 92.7 %all-gather.9.cloned.1.call-start = ((), (), s32[]{:S(2)}) async-start(), calls=%async_computation.5 | async-start | bytes 2359296 | tf_op jit(solution)/shard_map/all_gather | solution.py:52
  10.3 253.4 %all-reduce.6.cloned.1.call-start = ((), (), s32[]{:S(2)}) async-start(), calls=%async_computation.6 | async-start | bytes 8388608 | tf_op jit(solution)/shard_map/psum | solution.py:101
  17.1 14.9 %copy-start = (bf16[1024,2048]{1,0:T(8,128)(2,1)S(1)}, bf16[1024,2048]{1,0:T(8,128)(2,1)}, u32[]{:S(2)}) copy-start(bf16[1024,2048]{1,0:T(8,128)(2,1)} %param.15) | copy-start | bytes 12582916
  32.0 38.4 %copy-start.22 = (f32[1024]{0:T(1024)}, f32[1024]{0:T(1024)S(1)}, u32[]{:S(2)}) copy-start(f32[1024]{0:T(1024)S(1)} %broadcast_multiply_fusion.8) | copy-start | bytes 12292
  33.3 0.6 copy-start.26
  33.3 37.1 %copy-start.24 = (f32[1024]{0:T(1024)}, f32[1024]{0:T(1024)S(1)}, u32[]{:S(2)}) copy-start(f32[1024]{0:T(1024)S(1)} %fusion.47) | copy-start | bytes 12292
  33.6 38.7 %copy-start.29 = (f32[4,128]{1,0:T(4,128)}, f32[4,128]{1,0:T(4,128)S(1)}, u32[]{:S(2)}) copy-start(f32[4,128]{1,0:T(4,128)S(1)} %add.148) | copy-start | bytes 6148
  33.9 36.6 %copy-start.31 = (f32[1,2,8,128]{3,1,2,0:T(2,128)}, f32[1,2,8,128]{3,1,2,0:T(2,128)S(1)}, u32[]{:S(2)}) copy-start(f32[1,2,8,128]{3,1,2,0:T(2,128)S(1)} %copy.87) | copy-start | bytes 24580
  33.9 36.6 %copy-start.20 = (f32[1,2,8,128]{3,1,2,0:T(2,128)}, f32[1,2,8,128]{3,1,2,0:T(2,128)S(1)}, u32[]{:S(2)}) copy-start(f32[1,2,8,128]{3,1,2,0:T(2,128)S(1)} %copy.86) | copy-start | bytes 24580
  70.6 9.3 copy-start.12
  72.3 7.7 copy-start.10
  97.6 3.2 copy-start.6
  102.2 7.3 copy-start.36
  108.3 210.4 %all-gather.11.cloned.1.call-start = ((), (), s32[]{:S(2)}) async-start(), calls=%async_computation.7 | async-start | bytes 9437184 | tf_op jit(solution)/shard_map/all_gather | solution.py:53
  108.9 267.4 %all-gather.13.cloned.1.call-start = ((), (), s32[]{:S(2)}) async-start(), calls=%async_computation.8 | async-start | bytes 9437184 | tf_op jit(solution)/shard_map/all_gather | solution.py:54
  109.4 467.5 %all-reduce.8.cloned.1.call-start = ((), (), s32[]{:S(2)}) async-start(), calls=%async_computation.9 | async-start | bytes 8388608 | tf_op jit(solution)/shard_map/psum | solution.py:132
  109.5 209.1 %copy-start.34 = (f32[1,2,8,128]{3,1,2,0:T(2,128)}, f32[1,2,8,128]{3,1,2,0:T(2,128)S(1)}, u32[]{:S(2)}) copy-start(f32[1,2,8,128]{3,1,2,0:T(2,128)S(1)} %copy.90) | copy-start | bytes 24580
  263.6 5.0 copy-start.1
  263.7 5.9 copy-start.4
  396.8 2.0 copy-start.38
  421.8 300.4 %reduce-scatter.7.cloned.1.call-start = ((), (), s32[]{:S(2)}) async-start(), calls=%async_computation.11 | async-start | bytes 2359296 | tf_op jit(solution)/shard_map/reduce_scatter | solution.py:200
  577.0 7.7 copy-start.2
  577.0 7.7 copy-start.5
  577.0 8.3 copy-start.8
  584.6 6.2 copy-start.15
  596.5 3.2 copy-start.9
  603.3 359.0 %all-reduce.10.cloned.1.call-start = ((), (), s32[]{:S(2)}) async-start(), calls=%async_computation.14 | async-start | bytes 16777216 | tf_op jit(solution)/shard_map/psum | solution.py:108
  610.2 28.2 %slice-start = ((s8[8388608]{0:T(1024)(128)(4,1)}), s8[4194304]{0:T(1024)(128)(4,1)S(1)}, s32[]{:S(2)}) async-start(s8[8388608]{0:T(1024)(128)(4,1)} %bitcast.80), calls=%async_computation.15 | async-start | bytes 8388608
  622.4 15.9 %slice-start.1 = ((s8[8388608]{0:T(1024)(128)(4,1)}), s8[4194304]{0:T(1024)(128)(4,1)S(1)}, s32[]{:S(2)}) async-start(s8[8388608]{0:T(1024)(128)(4,1)} %bitcast.80), calls=%async_computation.16 | async-start | bytes 8388608
  638.4 7.1 copy-start.13
  642.9 11.2 copy-start.11
  642.9 11.2 copy-start.30
  660.9 11.0 copy-start.18
  672.0 364.3 %reduce-scatter.11.cloned.1.call-start = ((), (), s32[]{:S(2)}) async-start(), calls=%async_computation.13 | async-start | bytes 9437184 | tf_op jit(solution)/shard_map/reduce_scatter | solution.py:200
  688.5 0.7 copy-start.35
  688.5 423.2 %reduce-scatter.9.cloned.1.call-start = ((), (), s32[]{:S(2)}) async-start(), calls=%async_computation.12 | async-start | bytes 9437184 | tf_op jit(solution)/shard_map/reduce_scatter | solution.py:200
  704.7 1.2 copy-start.16
  704.7 1.6 copy-start.17
  704.7 1.9 copy-start.19
  704.7 1.9 copy-start.21
  704.7 1.9 copy-start.23
  704.7 1.9 copy-start.25
  704.7 1.9 copy-start.32
  704.7 14.5 %copy-start.28 = (f32[1,2,8,128]{3,2,1,0:T(8,128)S(1)}, f32[1,2,8,128]{3,2,1,0:T(8,128)}, u32[]{:S(2)}) copy-start(f32[1,2,8,128]{3,2,1,0:T(8,128)} %get-tuple-element.42) | copy-start | bytes 24580
  704.7 14.5 %copy-start.37 = (u32[32]{0:T(128)S(1)}, u32[32]{0:T(128)}, u32[]{:S(2)}) copy-start(u32[32]{0:T(128)} %constant.45) | copy-start | bytes 388
  704.8 15.1 %copy-start.33 = (f32[2048]{0:T(1024)S(1)}, f32[2048]{0:T(1024)}, u32[]{:S(2)}) copy-start(f32[2048]{0:T(1024)} %get-tuple-element.57) | copy-start | bytes 24580
  704.8 471.9 %reduce-scatter.5.cloned.1.call-start = ((), (), s32[]{:S(2)}) async-start(), calls=%async_computation.10 | async-start | bytes 7077888 | tf_op jit(solution)/shard_map/reduce_scatter | solution.py:200
  719.2 2.6 copy-start.14
  719.2 248.6 %copy-start.27 = (f32[1024]{0:T(1024)S(1)}, f32[1024]{0:T(1024)}, u32[]{:S(2)}) copy-start(f32[1024]{0:T(1024)} %copy-done.26) | copy-start | bytes 12292
  962.3 5.5 copy-start.3
  962.3 5.9 copy-start.7
Sparse Core Ops, SparseCore 0:
  10.4 49.4 all-gather.6
  61.8 28.0 all-gather.8
  108.4 155.2 all-reduce.5
  265.4 53.2 all-gather.10
  320.4 55.8 all-gather.12
  422.0 154.9 all-reduce.7
  603.5 40.0 reduce-scatter.6
  672.1 290.1 all-reduce.9
  965.8 70.4 reduce-scatter.10
  1040.2 71.4 reduce-scatter.8
  1115.1 61.6 reduce-scatter.4
where the time goes:
time: 1200 us; the launch traced here: 1190 us
  waiting for transfers between devices  797 us (66%)
  matrix products  197 us (16%)
  other arithmetic  103 us (9%)
  blocking collectives  36.5 us (3%)
  local copies, waits for them, and re-layouts  35.8 us (3%)
  between operations  16.4 us (1%)
    psum x1, waiting for transfers between devices, shards(): lax.psum(ffn_part.astype(jnp.bfloat16), 'mp').astype(jnp.float32)  238 us
    reduce_scatter x4, waiting for transfers between devices, scatter(): lax.psum_scatter(low, 'dp', scatter_dimension=axis, tiled=True)  153 us
    psum x1, waiting for transfers between devices, shards(): lax.psum(attn_part.astype(jnp.bfloat16), 'mp').astype(jnp.float32)  153 us
    psum x1, waiting for transfers between devices, shards(): lax.psum(two_part.astype(jnp.bfloat16), 'mp').astype(jnp.float32)  137 us
    all_gather x1, waiting for transfers between devices, shards(): whole_fc1 = lax.all_gather(w_fc1, 'dp', axis=0, tiled=True)  46.6 us
    all_gather x1, waiting for transfers between devices, shards(): whole_fc2 = lax.all_gather(w_fc2, 'dp', axis=1, tiled=True)  41.4 us
    all_gather x1, waiting for transfers between devices, shards(): whole_qkv = lax.all_gather(w_qkv, 'dp', axis=0, tiled=True)  26.1 us
    unnamed x1, blocking collectives  25.3 us
  transfers between devices with their start and end apart: 11, of which 9 were waited for; matrix products, arithmetic and copies ran while one was open for 21% of the time, Pallas kernels for 0%

commit v1 on v0

--- a/solution.py
+++ b/solution.py
@@ -7,6 +7,10 @@
 HEAD = 128
 EPS = 1e-05
 NEG = -1e30
+
+
+def works_settle(v0):
+    return lax.all_gather(v0, "mp").sum(axis=0)
 
 
 def layer_norm(values, gain_vec, shift_vec):
@@ -97,9 +101,7 @@
         .reshape(seq_rows, local_width)
     )
     attn_part = jnp.dot(mixed_heads, whole_out, preferred_element_type=jnp.float32)
-    residual = (
-        inputs + lax.psum(attn_part.astype(jnp.bfloat16), "mp").astype(jnp.float32) + bias_out
-    )
+    residual = inputs + works_settle(attn_part.astype(jnp.bfloat16)).astype(jnp.float32) + bias_out
     normed_two = layer_norm(residual, gain_two, shift_two).astype(jnp.bfloat16)
     preact = jnp.dot(normed_two, whole_fc1, preferred_element_type=jnp.float32) + bias_fc1
     activated = smooth_gate(preact).astype(jnp.bfloat16)

time: 1200 us -> 1320 us (1.10)
  waiting for transfers between devices: 797 us -> 915 us
    all_gather x0 -> x1, waiting for transfers between devices: none -> 285 us  [works_settle(): return lax.all_gather(v0, 'mp').sum(axis=0)]
    psum x1 -> x0, waiting for transfers between devices: 153 us -> none  [shards(): lax.psum(attn_part.astype(jnp.bfloat16), 'mp').astype(jnp.float32)]
    all_gather x1, waiting for transfers between devices: 46.6 us -> 33.4 us  [shards(): whole_fc1 = lax.all_gather(w_fc1, 'dp', axis=0, tiled=True)]
  transfers between devices with their start and end apart: 11 -> 11, of which waited for: 9 -> 9; matrix products, arithmetic and copies ran while one was open for 21% -> 20% of each run, Pallas kernels for 0% -> 0%
where the time goes in v1:
time: 1320 us; the launch traced here: 1310 us
  waiting for transfers between devices  915 us (69%)
  matrix products  187 us (14%)
  other arithmetic  115 us (9%)
  blocking collectives  36.5 us (3%)
  local copies, waits for them, and re-layouts  35.7 us (3%)
  between operations  16.4 us (1%)
    all_gather x1, waiting for transfers between devices, works_settle(): return lax.all_gather(v0, 'mp').sum(axis=0)  285 us
    psum x1, waiting for transfers between devices, shards(): lax.psum(ffn_part.astype(jnp.bfloat16), 'mp').astype(jnp.float32)  238 us
    reduce_scatter x4, waiting for transfers between devices, scatter(): lax.psum_scatter(low, 'dp', scatter_dimension=axis, tiled=True)  153 us
    psum x1, waiting for transfers between devices, shards(): lax.psum(two_part.astype(jnp.bfloat16), 'mp').astype(jnp.float32)  137 us
    all_gather x1, waiting for transfers between devices, shards(): whole_fc2 = lax.all_gather(w_fc2, 'dp', axis=1, tiled=True)  41.4 us
    all_gather x1, waiting for transfers between devices, shards(): whole_fc1 = lax.all_gather(w_fc1, 'dp', axis=0, tiled=True)  33.4 us
  transfers between devices with their start and end apart: 11, of which 9 were waited for; matrix products, arithmetic and copies ran while one was open for 20% of the time, Pallas kernels for 0%

profile of v1, /device:TPU:0, one launch (start us, length us, event | category | flops | bytes accessed | tf_op | source)
XLA Modules:
  0.0 1306.8 jit_solution(17185313752995946794)
XLA Ops:
  7.2 2.3 copy.59
  11.1 0.8 dynamic-update-slice.8
  11.9 0.8 dynamic-update-slice.9
  12.8 0.8 dynamic-update-slice.10
  13.6 0.8 dynamic-update-slice.11
  14.4 0.8 dynamic-update-slice.12
  17.1 11.2 all-gather.2
  29.2 2.8 convert_reduce_fusion.2
  32.0 1.2 fusion.18
  33.9 26.1 %all-gather.9.cloned.1.call-done = bf16[2048,3,512]{0,2,1:T(8,128)(2,1)} async-done(((bf16[256,3,512]{0,2,1:T(8,128)(2,1)}), bf16[2048,3,512]{0,2,1:T(8,128)(2,1)}) %all-gather.9.cloned.1.call-update) | async-done | bytes 6291472 | tf_op jit(solution)/shard_map/all_gather | solution.py:55
  60.0 10.4 fusion.43
  70.6 1.7 fusion.60
  72.3 7.7 fusion.62
  80.0 8.1 fusion
  88.1 2.0 copy.60
  90.1 7.4 divide_convert_fusion
  97.5 3.2 copy-done.6
  100.7 1.4 convolution_convert_fusion.3
  102.2 6.0 convolution_convert_fusion.2
  110.8 284.6 %all-gather.17.cloned.1.call-done = bf16[4096,2048]{1,0:T(8,128)(2,1)} async-done(((bf16[1024,2048]{1,0:T(8,128)(2,1)}), bf16[4096,2048]{1,0:T(8,128)(2,1)}) %all-gather.17.cloned.1.call-update) | async-done | bytes 16777232 | tf_op jit(solution)/shard_map/all_gather | solution.py:13
  395.3 12.4 reduce_sum.203
  407.8 5.0 fusion.26
  412.8 0.9 copy-done.4
  413.7 2.4 multiply_reduce_fusion.1
  416.1 33.4 %all-gather.13.cloned.1.call-done = bf16[2048,2048]{1,0:T(8,128)(2,1)} async-done(((bf16[256,2048]{1,0:T(8,128)(2,1)}), bf16[2048,2048]{1,0:T(8,128)(2,1)}) %all-gather.13.cloned.1.call-update) | async-done | bytes 8388624 | tf_op jit(solution)/shard_map/all_gather | solution.py:57
  449.6 16.2 %fusion.55 = f32[1024,2048]{1,0:T(8,128)} fusion(bf16[2048,2048]{1,0:T(8,128)(2,1)} %all-gather.13.cloned.1.call-done, f32[2048]{0:T(1024)S(1)} %bitcast.120, f32[2048]{0:T(1024)S(1)} %bitcast.111, f32[1024]{0:T(1024)S(1)} %fusion.48, bf16[1024,2048]{1,0:T(8,128)(2,1)} %reduce_sum.203, bf16[1024,2048]{1,0:T(8,128)(2,1)} %param.15, ...), kind=kOutput, calls=%fused_computation.131 | convolution fusion | flops 8608808960 | bytes 25198592 | tf_op jit(solution)/shard_map/dot_general | solution.py:106
  465.7 41.4 %all-gather.15.cloned.1.call-done = bf16[2048,2048]{1,0:T(8,128)(2,1)} async-done(((bf16[2048,256]{1,0:T(8,128)(2,1)}), bf16[2048,2048]{1,0:T(8,128)(2,1)}) %all-gather.15.cloned.1.call-update) | async-done | bytes 8388624 | tf_op jit(solution)/shard_map/all_gather | solution.py:58
  507.2 20.7 %fusion.63 = (f32[2048]{0:T(1024)}, bf16[1024,2048]{1,0:T(8,128)(2,1)S(1)}) fusion(f32[1024,2048]{1,0:T(8,128)} %fusion.55, f32[2048]{0:T(1024)S(1)} %bitcast.122, bf16[2048,2048]{1,0:T(8,128)(2,1)} %all-gather.15.cloned.1.call-done, bf16[1024,2048]{1,0:T(8,128)(2,1)} %param.16, pred[1024]{0:T(1024)(128)(4,1)S(1)} %iota_compare_fusion.1), kind=kOutput, calls=%fused_computation.137 | convolution fusion | flops 8642361344 | bytes 25183232 | tf_op jit(solution)/shard_map/sd,fd->sf/dot_general | solution.py:124
  527.9 2.1 copy-done.38
  529.9 12.6 convolution_convert_fusion
  544.0 17.2 %convolution_convert_fusion.1 = bf16[1024,2048]{1,0:T(8,128)(2,1)} fusion(bf16[2048,2048]{1,0:T(8,128)(2,1)} %all-gather.15.cloned.1.call-done, f32[1024,2048]{1,0:T(8,128)} %fusion.55, f32[2048]{0:T(1024)S(1)} %bitcast.123), kind=kOutput, calls=%fused_computation.62 | convolution fusion | flops 8613003264 | bytes 20979712 | tf_op jit(solution)/shard_map/dot_general | solution.py:108
  561.2 136.6 %all-reduce.5.cloned.1.call-done = bf16[1024,2048]{1,0:T(8,128)(2,1)} async-done(((bf16[1024,2048]{1,0:T(8,128)(2,1)}), bf16[1024,2048]{1,0:T(8,128)(2,1)}) %all-reduce.5.cloned.1.call-update) | async-done | bytes 4194320 | tf_op jit(solution)/shard_map/psum | solution.py:134
  697.7 7.6 convert_reduce_fusion.1
  706.0 5.5 fusion.21
  711.5 5.7 fusion.59
  717.2 3.2 copy-done.9
  720.4 3.6 multiply_convert_fusion.5
  724.3 6.3 fusion.39
  730.6 12.3 multiply_reduce_fusion
  742.9 16.0 %multiply_convert_fusion.2 = bf16[4,1024,1024]{1,2,0:T(8,128)(2,1)} fusion(f32[4,1024,1024]{1,2,0:T(8,128)} %get-tuple-element.54, f32[4,1024,1024]{1,2,0:T(8,128)} %get-tuple-element.50, f32[4,1024]{1,0:T(4,128)S(1)} %get-tuple-element.53, f32[4,1024]{1,0:T(4,128)S(1)} %log_add_fusion), kind=kLoop, calls=%fused_computation.2 | loop fusion | flops 16777216 | bytes 41975808 | tf_op jit(solution)/shard_map/convert_element_type | solution.py:156
  758.9 4.6 bitcast_convert_fusion.1
  763.5 2.4 copy.71
  765.9 6.4 bitcast_convert_fusion.2
  772.3 2.3 copy.69
  774.6 6.3 multiply_convert_fusion.6
  781.4 11.1 bitcast_convert_fusion
  792.6 16.5 %multiply_convert_fusion = bf16[2048,2048]{1,0:T(8,128)(2,1)} fusion(f32[]{:T(128)S(6)} %div.63, bf16[1024,2048]{1,0:T(8,128)(2,1)} %param.16, pred[1024]{0:T(1024)(128)(4,1)S(1)} %iota_compare_fusion.1, f32[1024,2048]{1,0:T(8,128)} %fusion.55, f32[2048]{0:T(1024)S(1)} %bitcast.124), kind=kOutput, calls=%fused_computation | convolution fusion | flops 8625586176 | bytes 20980740 | tf_op jit(solution)/shard_map/sf,sd->fd/dot_general | solution.py:120
  809.8 15.5 %multiply_convert_fusion.1 = bf16[2048,2048]{1,0:T(8,128)(2,1)} fusion(f32[]{:T(128)S(6)} %div.63, bf16[1024,2048]{1,0:T(8,128)(2,1)} %copy-done.38, f32[2048]{0:T(1024)S(1)} %bitcast.121, f32[2048]{0:T(1024)S(1)} %bitcast.115, f32[1024]{0:T(1024)S(1)} %fusion.48, bf16[1024,2048]{1,0:T(8,128)(2,1)} %reduce_sum.203, bf16[1024,2048]{1,0:T(8,128)(2,1)} %param.15, ...), kind=kOutput, calls=%fused_computation.1 | convolution fusion | flops 8617197568 | bytes 21004292 | tf_op jit(solution)/shard_map/sd,sf->df/dot_general | solution.py:130
  825.4 1.1 copy-done.16
  827.2 12.6 multiply_convert_fusion.3
  840.6 1.8 bitcast_reduce_fusion
  842.9 1.8 convert_element_type.146
  844.6 238.3 %all-reduce.7.cloned.1.call-done = (bf16[1024,2048]{1,0:T(8,128)(2,1)}, bf16[1024,2048]{1,0:T(8,128)(2,1)}) async-done(((bf16[1024,2048]{1,0:T(8,128)(2,1)}, bf16[1024,2048]{1,0:T(8,128)(2,1)}), (bf16[1024,2048]{1,0:T(8,128)(2,1)}, bf16[1024,2048]{1,0:T(8,128)(2,1)})) %all-reduce.7.cloned.1.call-update) | async-done | bytes 8388624 | tf_op jit(solution)/shard_map/psum | solution.py:110
  1082.9 5.5 convert_reduce_fusion
  1088.8 4.5 fusion.22
  1093.4 25.3 %all-reduce = f32[8,1920]{1,0:T(8,128)S(1)} all-reduce(f32[8,1920]{1,0:T(8,128)S(1)} %constant_dynamic-update-slice_fusion), channel_id=8, replica_groups=mesh['dp'=8,'mp'=4] {'dp'}, use_global_device_ids=true, to_apply=%region_30.31.clone | all-reduce | flops 15360 | bytes 122880
  1120.1 36.7 %reduce-scatter.11.cloned.1.call-done = bf16[2048,256]{1,0:T(8,128)(2,1)} async-done(((bf16[2048,2048]{1,0:T(8,128)(2,1)}), bf16[2048,256]{1,0:T(8,128)(2,1)}) %reduce-scatter.11.cloned.1.call-update) | async-done | bytes 1048592 | tf_op jit(solution)/shard_map/reduce_scatter | solution.py:202
  1156.8 2.7 convert_element_type.150
  1159.6 72.7 %reduce-scatter.9.cloned.1.call-done = bf16[256,2048]{1,0:T(8,128)(2,1)} async-done(((bf16[2048,2048]{1,0:T(8,128)(2,1)}), bf16[256,2048]{1,0:T(8,128)(2,1)}) %reduce-scatter.9.cloned.1.call-update) | async-done | bytes 1048592 | tf_op jit(solution)/shard_map/reduce_scatter | solution.py:202
  1232.3 2.8 convert_element_type.148
  1235.0 1.3 fusion.61
  1236.4 17.6 %add_add_fusion.2 = (f32[1024,2048]{1,0:T(8,128)}, bf16[1024,2048]{1,0:T(8,128)(2,1)}) fusion(f32[1024,2048]{1,0:T(8,128)} %copy-done.9, bf16[1024,2048]{1,0:T(8,128)(2,1)} %param.15, bf16[1024,2048]{1,0:T(8,128)(2,1)} %get-tuple-element.27, f32[1024]{0:T(1024)S(1)} %negate_multiply_fusion, f32[1024]{0:T(1024)S(1)} %multiply_multiply_fusion.2, ...), kind=kLoop, calls=%fused_computation.46 | loop fusion | flops 35651584 | bytes 37789696 | tf_op jit(solution)/shard_map/add | solution.py:178
  1253.9 43.4 %reduce-scatter.5.cloned.1.call-done = bf16[256,3,512]{2,0,1:T(8,128)(2,1)} async-done(((bf16[2048,3,512]{2,0,1:T(8,128)(2,1)}), bf16[256,3,512]{2,0,1:T(8,128)(2,1)}) %reduce-scatter.5.cloned.1.call-update) | async-done | bytes 786448 | tf_op jit(solution)/shard_map/reduce_scatter | solution.py:202
  1297.3 2.5 convert_element_type.144
  (163 shorter events, 13.6 us)
Async XLA Ops:
  7.2 52.8 %all-gather.9.cloned.1.call-start = ((), (), s32[]{:S(2)}) async-start(), calls=%async_computation.4 | async-start | bytes 7077888 | tf_op jit(solution)/shard_map/all_gather | solution.py:55
  9.5 92.6 %all-gather.11.cloned.1.call-start = ((), (), s32[]{:S(2)}) async-start(), calls=%async_computation.5 | async-start | bytes 2359296 | tf_op jit(solution)/shard_map/all_gather | solution.py:56
  10.3 385.0 %all-gather.17.cloned.1.call-start = ((), (), s32[]{:S(2)}) async-start(), calls=%async_computation.13 | async-start | bytes 20971520 | tf_op jit(solution)/shard_map/all_gather | solution.py:13
  17.1 14.9 %copy-start = (bf16[1024,2048]{1,0:T(8,128)(2,1)S(1)}, bf16[1024,2048]{1,0:T(8,128)(2,1)}, u32[]{:S(2)}) copy-start(bf16[1024,2048]{1,0:T(8,128)(2,1)} %param.15) | copy-start | bytes 12582916
  32.0 38.4 %copy-start.22 = (f32[1024]{0:T(1024)}, f32[1024]{0:T(1024)S(1)}, u32[]{:S(2)}) copy-start(f32[1024]{0:T(1024)S(1)} %broadcast_multiply_fusion.8) | copy-start | bytes 12292
  33.3 0.6 copy-start.26
  33.3 37.1 %copy-start.24 = (f32[1024]{0:T(1024)}, f32[1024]{0:T(1024)S(1)}, u32[]{:S(2)}) copy-start(f32[1024]{0:T(1024)S(1)} %fusion.47) | copy-start | bytes 12292
  33.6 38.7 %copy-start.29 = (f32[4,128]{1,0:T(4,128)}, f32[4,128]{1,0:T(4,128)S(1)}, u32[]{:S(2)}) copy-start(f32[4,128]{1,0:T(4,128)S(1)} %add.146) | copy-start | bytes 6148
  33.9 36.6 %copy-start.31 = (f32[1,2,8,128]{3,1,2,0:T(2,128)}, f32[1,2,8,128]{3,1,2,0:T(2,128)S(1)}, u32[]{:S(2)}) copy-start(f32[1,2,8,128]{3,1,2,0:T(2,128)S(1)} %copy.87) | copy-start | bytes 24580
  33.9 36.6 %copy-start.20 = (f32[1,2,8,128]{3,1,2,0:T(2,128)}, f32[1,2,8,128]{3,1,2,0:T(2,128)S(1)}, u32[]{:S(2)}) copy-start(f32[1,2,8,128]{3,1,2,0:T(2,128)S(1)} %copy.86) | copy-start | bytes 24580
  70.6 9.3 copy-start.12
  72.3 7.7 copy-start.10
  97.5 3.2 copy-start.6
  102.2 7.3 copy-start.36
  108.2 341.4 %all-gather.13.cloned.1.call-start = ((), (), s32[]{:S(2)}) async-start(), calls=%async_computation.6 | async-start | bytes 9437184 | tf_op jit(solution)/shard_map/all_gather | solution.py:57
  108.8 398.4 %all-gather.15.cloned.1.call-start = ((), (), s32[]{:S(2)}) async-start(), calls=%async_computation.7 | async-start | bytes 9437184 | tf_op jit(solution)/shard_map/all_gather | solution.py:58
  109.4 588.4 %all-reduce.5.cloned.1.call-start = ((), (), s32[]{:S(2)}) async-start(), calls=%async_computation.8 | async-start | bytes 8388608 | tf_op jit(solution)/shard_map/psum | solution.py:134
  109.4 340.1 %copy-start.34 = (f32[1,2,8,128]{3,1,2,0:T(2,128)}, f32[1,2,8,128]{3,1,2,0:T(2,128)S(1)}, u32[]{:S(2)}) copy-start(f32[1,2,8,128]{3,1,2,0:T(2,128)S(1)} %copy.90) | copy-start | bytes 24580
  407.8 5.0 copy-start.1
  407.8 5.9 copy-start.4
  527.9 2.1 copy-start.38
  542.6 300.3 %reduce-scatter.7.cloned.1.call-start = ((), (), s32[]{:S(2)}) async-start(), calls=%async_computation.10 | async-start | bytes 2359296 | tf_op jit(solution)/shard_map/reduce_scatter | solution.py:202
  697.7 7.7 copy-start.2
  697.7 7.7 copy-start.5
  697.7 8.3 copy-start.8
  705.4 6.1 copy-start.15
  717.2 3.2 copy-start.9
  724.1 358.9 %all-reduce.7.cloned.1.call-start = ((), (), s32[]{:S(2)}) async-start(), calls=%async_computation.14 | async-start | bytes 16777216 | tf_op jit(solution)/shard_map/psum | solution.py:110
  730.6 28.2 %slice-start = ((s8[8388608]{0:T(1024)(128)(4,1)}), s8[4194304]{0:T(1024)(128)(4,1)S(1)}, s32[]{:S(2)}) async-start(s8[8388608]{0:T(1024)(128)(4,1)} %bitcast.81), calls=%async_computation.15 | async-start | bytes 8388608
  742.9 16.0 %slice-start.1 = ((s8[8388608]{0:T(1024)(128)(4,1)}), s8[4194304]{0:T(1024)(128)(4,1)S(1)}, s32[]{:S(2)}) async-start(s8[8388608]{0:T(1024)(128)(4,1)} %bitcast.81), calls=%async_computation.16 | async-start | bytes 8388608
  758.9 7.0 copy-start.13
  763.5 11.1 copy-start.11
  763.5 11.1 copy-start.30
  781.4 11.1 copy-start.18
  792.6 364.3 %reduce-scatter.11.cloned.1.call-start = ((), (), s32[]{:S(2)}) async-start(), calls=%async_computation.12 | async-start | bytes 9437184 | tf_op jit(solution)/shard_map/reduce_scatter | solution.py:202
  809.1 0.7 copy-start.35
  809.1 423.1 %reduce-scatter.9.cloned.1.call-start = ((), (), s32[]{:S(2)}) async-start(), calls=%async_computation.11 | async-start | bytes 9437184 | tf_op jit(solution)/shard_map/reduce_scatter | solution.py:202
  825.3 1.2 copy-start.16
  825.3 1.6 copy-start.17
  825.3 1.9 copy-start.19
  825.3 1.9 copy-start.21
  825.3 1.9 copy-start.23
  825.3 1.9 copy-start.25
  825.3 1.9 copy-start.32
  825.4 14.5 %copy-start.28 = (f32[1,2,8,128]{3,2,1,0:T(8,128)S(1)}, f32[1,2,8,128]{3,2,1,0:T(8,128)}, u32[]{:S(2)}) copy-start(f32[1,2,8,128]{3,2,1,0:T(8,128)} %get-tuple-element.42) | copy-start | bytes 24580
  825.4 14.5 %copy-start.37 = (u32[32]{0:T(128)S(1)}, u32[32]{0:T(128)}, u32[]{:S(2)}) copy-start(u32[32]{0:T(128)} %constant.47) | copy-start | bytes 388
  825.4 15.1 %copy-start.33 = (f32[2048]{0:T(1024)S(1)}, f32[2048]{0:T(1024)}, u32[]{:S(2)}) copy-start(f32[2048]{0:T(1024)} %get-tuple-element.57) | copy-start | bytes 24580
  825.4 471.9 %reduce-scatter.5.cloned.1.call-start = ((), (), s32[]{:S(2)}) async-start(), calls=%async_computation.9 | async-start | bytes 7077888 | tf_op jit(solution)/shard_map/reduce_scatter | solution.py:202
  839.8 2.6 copy-start.14
  839.8 248.6 %copy-start.27 = (f32[1024]{0:T(1024)S(1)}, f32[1024]{0:T(1024)}, u32[]{:S(2)}) copy-start(f32[1024]{0:T(1024)} %copy-done.26) | copy-start | bytes 12292
  1082.9 5.6 copy-start.3
  1082.9 5.9 copy-start.7
Sparse Core Ops, SparseCore 0:
  10.4 49.4 all-gather.8
  61.8 28.0 all-gather.10
  108.3 286.9 all-gather.16
  397.1 52.4 all-gather.12
  451.3 55.8 all-gather.14
  542.7 154.9 all-reduce.4
  724.2 40.0 reduce-scatter.6
  792.7 290.1 all-reduce.6
  1086.4 70.4 reduce-scatter.10
  1160.7 71.4 reduce-scatter.8
  1235.6 61.6 reduce-scatter.4
